TPU v7x, 32 devices: a whole 2x2x4 slice. The times are simulated.
32 devices in a mesh: beta: 16 (over z, y, x), grp: 2 (over core).
Axes of the slice: x: 2, y: 2, z: 4, core: 2. Of those that a mesh axis runs over, the one named last changes fastest.
Arguments:
- samples: float32 [128, 8, 128, 128], P('beta', 'grp'), parts along dimension 1, may hold values from -6 to 6
Outputs:
- coeffs: float32 [128, 2, 8, 64, 64], P('beta', None, 'grp'), parts along dimension 2
- power: float32 [8, 64], P('grp'), parts along dimension 0
There are 2 independent parts, one for each index of `grp`. A program takes and returns all parts, laid end to end along the dimension named above; each array names one. Nothing has to cross between parts.
All inputs are finite; a program needn't handle non-finite values.
Results may differ from a plain program's by a relative error of at most 0.0003.
Values sent between devices are 32-bit elements; how exact they have to be, the bound alone decides.
No kernel may reach another device: no remote copies, remote signals or barrier semaphores. Data moves between devices by JAX's collectives and lax.ppermute only.
A program may use at most 64 MiB of HBM per device.

v0:
```python
import jax
import jax.numpy as jnp
from jax import lax
from jax.sharding import PartitionSpec as P

HIGHEST = lax.Precision.HIGHEST


def beta_angles(spread):
    grid_size = 2 * spread
    return (2.0 * jnp.arange(grid_size, dtype=jnp.float32) + 1.0) * (jnp.pi / (4.0 * spread))


def quadrature(spread):
    angles = beta_angles(spread)
    odd_terms = 2.0 * jnp.arange(spread, dtype=jnp.float32) + 1.0
    series = jnp.sum(jnp.sin(angles[:, None] * odd_terms[None, :]) / odd_terms[None, :], axis=1)
    return 2.0 / spread * jnp.sin(angles) * series


def gamma_table(spread):
    grid_size = 2 * spread
    positions = jnp.arange(grid_size, dtype=jnp.int32)
    orders = jnp.arange(spread, dtype=jnp.int32)
    phase_index = positions[:, None] * orders[None, :] % grid_size
    angles = phase_index.astype(jnp.float32) * (2.0 * jnp.pi / grid_size)
    return jnp.concatenate([jnp.cos(angles), -jnp.sin(angles)], axis=1)


def alpha_table(spread, row_index):
    grid_size = 2 * spread
    positions = jnp.arange(grid_size, dtype=jnp.int32)
    phase_index = row_index[:, None] * positions[None, :] % grid_size
    angles = phase_index.astype(jnp.float32) * (2.0 * jnp.pi / grid_size)
    cosine = jnp.cos(angles) / grid_size
    sine_part = jnp.sin(angles) / grid_size
    real_rows = jnp.stack([cosine, sine_part], axis=1)
    imag_rows = jnp.stack([-sine_part, cosine], axis=1)
    return jnp.stack([real_rows, imag_rows], axis=0)


def log_factorial(value, float_type):
    return lax.lgamma((value + 1).astype(float_type))


def wigner_start(alpha_order, gamma_order, log_cosine, log_sine):
    float_type = log_cosine.dtype
    lowest = jnp.maximum(jnp.abs(alpha_order), gamma_order)
    shift_low = jnp.maximum(0, gamma_order - alpha_order)
    magnitude = 0.5 * (
        log_factorial(lowest + alpha_order, float_type)
        + log_factorial(lowest - alpha_order, float_type)
        + log_factorial(lowest + gamma_order, float_type)
        + log_factorial(lowest - gamma_order, float_type)
    )
    magnitude = (
        magnitude
        - log_factorial(lowest + gamma_order - shift_low, float_type)
        - log_factorial(shift_low, float_type)
    )
    magnitude = magnitude - log_factorial(alpha_order - gamma_order + shift_low, float_type)
    magnitude = magnitude - log_factorial(lowest - alpha_order - shift_low, float_type)
    cos_power = (2 * lowest + gamma_order - alpha_order - 2 * shift_low).astype(float_type)
    sin_power = (alpha_order - gamma_order + 2 * shift_low).astype(float_type)
    parity = (alpha_order - gamma_order + shift_low) % 2
    sign_factor = (1 - 2 * parity).astype(float_type)
    return sign_factor * jnp.exp(magnitude + cos_power * log_cosine + sin_power * log_sine)


def advance(degree, carried, alpha_order, gamma_order, cos_angles, start_value, lowest):
    former, current = carried
    float_type = current.dtype
    previous = (degree - 1).astype(float_type)
    alpha_float = alpha_order.astype(float_type)
    gamma_float = gamma_order.astype(float_type)
    cross_ratio = alpha_float * gamma_float / jnp.maximum(previous * (previous + 1.0), 1.0)
    upper_term = ((previous + 1.0) * (previous + 1.0) - alpha_float * alpha_float) * (
        (previous + 1.0) * (previous + 1.0) - gamma_float * gamma_float
    )
    lower_term = (previous * previous - alpha_float * alpha_float) * (
        previous * previous - gamma_float * gamma_float
    )
    root_upper = jnp.sqrt(jnp.maximum(upper_term, 1.0))
    forward = (previous + 1.0) * (2.0 * previous + 1.0) / root_upper
    backward = (
        (previous + 1.0)
        * jnp.sqrt(jnp.maximum(lower_term, 0.0))
        / (jnp.maximum(previous, 1.0) * root_upper)
    )
    recurred = forward * (cos_angles - cross_ratio) * current - backward * former
    renewed = jnp.where(degree == lowest, start_value, recurred)
    return (current, renewed)


def degree_rows(row_index, weighted, spread):
    stride = 8
    grid_size = 2 * spread
    group_size = row_index.shape[0]
    channels = weighted.shape[2]
    block_count = spread // stride
    alpha_order = jnp.where(row_index < spread, row_index, row_index - grid_size)[:, None, None]
    gamma_order = jnp.arange(spread, dtype=jnp.int32)[None, None, :]
    angles = beta_angles(spread)
    cos_angles = jnp.cos(angles)[None, :, None]
    log_cosine = jnp.log(jnp.cos(0.5 * angles))[None, :, None]
    log_sine = jnp.log(jnp.sin(0.5 * angles))[None, :, None]
    lowest = jnp.maximum(jnp.abs(alpha_order), gamma_order)
    start_value = wigner_start(alpha_order, gamma_order, log_cosine, log_sine)
    first_block = jnp.min(jnp.abs(alpha_order)) // stride
    empty_state = jnp.zeros((group_size, grid_size, spread), jnp.float32)

    def compute_block(operands):
        block_index, former, current = operands
        levels = []
        for offset in range(stride):
            former, current = advance(
                block_index * stride + offset,
                (former, current),
                alpha_order,
                gamma_order,
                cos_angles,
                start_value,
                lowest,
            )
            levels.append(current)
        stacked = jnp.stack(levels, axis=0)
        block_part = jnp.einsum("jgkq,kgcq->gcjq", stacked, weighted, precision=HIGHEST)
        return (former, current, block_part)

    def skip_block(operands):
        block_index, former, current = operands
        return (former, current, jnp.zeros((group_size, channels, stride, spread), jnp.float32))

    def block_step(carried, block_index):
        former, current = carried
        former, current, block_part = lax.cond(
            block_index >= first_block, compute_block, skip_block, (block_index, former, current)
        )
        return ((former, current), block_part)

    _, parts = lax.scan(
        block_step, (empty_state, empty_state), jnp.arange(block_count, dtype=jnp.int32)
    )
    output = jnp.transpose(parts, (1, 2, 0, 3, 4)).reshape(group_size, channels, spread, spread)
    degree_scale = 8.0 * jnp.sqrt(2.0 * jnp.arange(spread, dtype=jnp.float32) + 1.0)
    return output * degree_scale[None, None, :, None]


def degree_energy(coeffs, functions, spread):
    split_view = coeffs.reshape(coeffs.shape[0], 2, functions, spread, spread)
    multiplicity = jnp.where(jnp.arange(spread) == 0, 1.0, 2.0).astype(jnp.float32)
    energy_sum = jnp.sum(split_view * split_view * multiplicity, axis=(0, 1, 4))
    degrees = 2.0 * jnp.arange(spread, dtype=jnp.float32) + 1.0
    return energy_sum / (degrees * degrees)[None, :]


def local(samples):
    devices = lax.axis_size("beta")
    device = lax.axis_index("beta")
    local_beta = samples.shape[0]
    functions = samples.shape[1]
    grid_size = samples.shape[2]
    spread = grid_size // 2
    channels = 2 * functions
    row_count = grid_size // devices
    natural_rows = jnp.arange(grid_size, dtype=jnp.int32)
    halfway = jnp.einsum("kfag,gx->kfax", samples, gamma_table(spread), precision=HIGHEST)
    halfway = halfway.reshape(local_beta, functions, grid_size, 2, spread)
    spectrum = jnp.einsum(
        "kfacq,spca->kpsfq", halfway, alpha_table(spread, natural_rows), precision=HIGHEST
    )
    spectrum = spectrum.reshape(local_beta, grid_size, channels, spread)
    received = lax.all_to_all(spectrum, "beta", split_axis=1, concat_axis=0, tiled=True)
    weighted = received * quadrature(spread)[:, None, None, None]
    owned_rows = lax.dynamic_slice_in_dim(natural_rows, device * row_count, row_count)
    computed = degree_rows(owned_rows, weighted, spread)
    power_part = degree_energy(computed, functions, spread)
    coeffs = computed
    power = lax.psum(power_part, "beta")
    coeffs = coeffs.reshape(row_count, 2, functions, spread, spread)
    return (coeffs, power)


def solution(mesh):
    return jax.shard_map(
        local,
        mesh=mesh,
        in_specs=(P("beta", "grp", None, None),),
        out_specs=(P("beta", None, "grp", None, None), P("grp", None)),
        check_vma=False,
    )
```

profile of v0, /device:TPU:0, one launch (start us, length us, event | category | flops | bytes accessed | tf_op | source)
XLA Modules:
  0.0 345.6 jit_solution(5608972519271680303)
XLA Ops:
  7.7 5.6 %copy.58 = f32[8,128,8,64]{3,2,0,1:T(8,128)} copy(f32[8,128,8,64]{1,3,2,0:T(8,128)} %bitcast.233) | data formatting | bytes 4194304 | tf_op jit(solution)/shard_map/reshape | solution.py:172
  13.3 5.5 %reshape.2457 = f32[16,1,32768]{2,1,0:T(1,128)} reshape(f32[128,8,8,64]{3,2,1,0:T(8,128)} %bitcast.230) | data formatting | bytes 4194304
  18.8 8.4 %all-to-all-start = ((f32[16,1,32768]{2,1,0:T(1,128)}), f32[16,1,32768]{2,1,0:T(1,128)}, u32[]{:S(2)}, u32[]{:S(2)}) async-start(f32[16,1,32768]{2,1,0:T(1,128)} %reshape.2457), calls=%async_computation | async-start | bytes 4194304 | tf_op jit(solution)/shard_map/all_to_all | solution.py:173
  32.1 38.1 %all-to-all-done = f32[16,1,32768]{2,1,0:T(1,128)} async-done(((f32[16,1,32768]{2,1,0:T(1,128)}), f32[16,1,32768]{2,1,0:T(1,128)}, u32[]{:S(2)}, u32[]{:S(2)}) %all-to-all-start) | async-done | bytes 2097184 | tf_op jit(solution)/shard_map/all_to_all | solution.py:173
  70.9 8.6 %reduce.3 = f32[16,32768]{1,0:T(8,128)} reduce(f32[16,1,32768]{2,1,0:T(1,128)} %all-to-all-done, f32[]{:T(128)} %broadcast.2681), dimensions={1}, to_apply=%all_to_all.13.reduce_sub_computation | reduce | bytes 4194308 | tf_op jit(solution)/shard_map/all_to_all | solution.py:173
  79.5 4.2 %reshape.2458 = f32[128,8,8,64]{3,2,1,0:T(8,128)} reshape(f32[16,32768]{1,0:T(8,128)} %reduce.3) | data formatting | bytes 4194304
  88.8 5.0 %copy.61 = f32[128,8,8,64]{0,2,3,1:T(8,128)} copy(f32[128,8,8,64]{3,2,1,0:T(8,128)} %bitcast_multiply_fusion) | data formatting | bytes 4194304
  93.9 182.8 %while.16 = (s32[]{:T(128)}, f32[8,128,64]{1,2,0:T(8,128)S(1)}, f32[8,128,64]{1,2,0:T(8,128)S(1)}, f32[8,8,8,8,64]{2,3,4,1,0:T(8,128)}, s32[8]{0:T(128)S(1)}, /*...) while((s32[]{:T(128)}, f32[8,128,64]{1,2,0:T(8,128)S(1)}, ...), condition=%wide.region_5.6_spmd.clone.clone, body=%wide.region_2.5_spmd.clone.clone.sunk | while | flops 53850804 | bytes 15474387 | solution.py:141
  95.2 18.6 %conditional.4 = (f32[8,128,64]{1,2,0:T(8,128)S(1)}, f32[8,128,64]{1,2,0:T(8,128)S(1)}, f32[1,8,8,8,64]{2,3,4,1,0:T(8,128)}) conditional(s32[]{:T(128)} %convert_element_type.412, (f32[8,128,64]{1,2,0:T(8,128)S(1)}, f32[8,128,64]{1,2,0:T(8,128)S(1)}) %tuple.139, (s32[]{:T(128)}, s32[8]{0:T(128)S(1)}, s32[8,1,1]{0,2,1:T(1,128)S(1)}, ...), branch_computations={%region_3.3_spmd, %region_4.4_spmd.clone} | conditional | flops 53850800 | bytes 11276004 | solution.py:136
  97.1 3.6 %fusion.11 = (f32[8,128,64]{1,2,0:T(8,128)S(1)}, f32[8,128,64]{1,2,0:T(8,128)S(1)}, f32[8,128,64]{1,2,0:T(8,128)S(1)}, f32[8,128,64]{1,2,0:T(8,128)S(1)}, f32[8,...) fusion(f32[128]{0:T(128)S(1)} %get-tuple-element.437, ...), kind=kLoop, calls=%fused_computation.9 | loop fusion | flops 3473408 | bytes 2684416 | tf_op jit(solution)/shard_map/while/body/eval_jaxpr/cond/branch_1_fun/jit(_where)/select_n | solution.py:91
  100.7 6.2 %stack.51 = f32[8,8,128,64]{2,0,3,1:T(8,128)} concatenate(f32[1,8,128,64]{2,0,3,1:T(1,128)} %bitcast.229, f32[1,8,128,64]{2,0,3,1:T(1,128)} %bitcast.228, f32[1,8,128,64]{2,0,3,1:T(1,128)} %bitcast.227, f32[1,8,128,64]{2,0,3,1:T(1,128)S(1)} %bitcast.226, f32[1,8,128,64]{2,0,3,1:T(1,128)S(1)} %bitcast.225, f32[1,8,128,64]{2,0,3,1:T(1,128)S(1)} %bitcast.224, ...), dimensions={0} | concatenate | bytes 4194304 | tf_op jit(solution)/shard_map/while/body/eval_jaxpr/cond/branch_1_fun/stack | solution.py:126
  106.9 6.9 %convolution_bitcast_fusion = f32[1,8,8,8,64]{2,3,4,1,0:T(8,128)} fusion(f32[8,8,128,64]{2,0,3,1:T(8,128)} %stack.51, f32[128,8,8,64]{0,2,3,1:T(8,128)} %get-tuple-element.428), kind=kOutput, calls=%fused_computation.4 | convolution fusion | flops 50331648 | bytes 4325376 | tf_op jit(solution)/shard_map/while/body/eval_jaxpr/cond/branch_1_fun/jgkq,kgcq->gcjq/dot_general | solution.py:127
  118.1 18.6 %conditional.4 = (f32[8,128,64]{1,2,0:T(8,128)S(1)}, f32[8,128,64]{1,2,0:T(8,128)S(1)}, f32[1,8,8,8,64]{2,3,4,1,0:T(8,128)}) conditional(s32[]{:T(128)} %convert_element_type.412, (f32[8,128,64]{1,2,0:T(8,128)S(1)}, f32[8,128,64]{1,2,0:T(8,128)S(1)}) %tuple.139, (s32[]{:T(128)}, s32[8]{0:T(128)S(1)}, s32[8,1,1]{0,2,1:T(1,128)S(1)}, ...), branch_computations={%region_3.3_spmd, %region_4.4_spmd.clone} | conditional | flops 53850800 | bytes 11276004 | solution.py:136
  119.9 3.6 %fusion.11 = (f32[8,128,64]{1,2,0:T(8,128)S(1)}, f32[8,128,64]{1,2,0:T(8,128)S(1)}, f32[8,128,64]{1,2,0:T(8,128)S(1)}, f32[8,128,64]{1,2,0:T(8,128)S(1)}, f32[8,...) fusion(f32[128]{0:T(128)S(1)} %get-tuple-element.437, ...), kind=kLoop, calls=%fused_computation.9 | loop fusion | flops 3473408 | bytes 2684416 | tf_op jit(solution)/shard_map/while/body/eval_jaxpr/cond/branch_1_fun/jit(_where)/select_n | solution.py:91
  123.5 6.2 %stack.51 = f32[8,8,128,64]{2,0,3,1:T(8,128)} concatenate(f32[1,8,128,64]{2,0,3,1:T(1,128)} %bitcast.229, f32[1,8,128,64]{2,0,3,1:T(1,128)} %bitcast.228, f32[1,8,128,64]{2,0,3,1:T(1,128)} %bitcast.227, f32[1,8,128,64]{2,0,3,1:T(1,128)S(1)} %bitcast.226, f32[1,8,128,64]{2,0,3,1:T(1,128)S(1)} %bitcast.225, f32[1,8,128,64]{2,0,3,1:T(1,128)S(1)} %bitcast.224, ...), dimensions={0} | concatenate | bytes 4194304 | tf_op jit(solution)/shard_map/while/body/eval_jaxpr/cond/branch_1_fun/stack | solution.py:126
  129.7 6.9 %convolution_bitcast_fusion = f32[1,8,8,8,64]{2,3,4,1,0:T(8,128)} fusion(f32[8,8,128,64]{2,0,3,1:T(8,128)} %stack.51, f32[128,8,8,64]{0,2,3,1:T(8,128)} %get-tuple-element.428), kind=kOutput, calls=%fused_computation.4 | convolution fusion | flops 50331648 | bytes 4325376 | tf_op jit(solution)/shard_map/while/body/eval_jaxpr/cond/branch_1_fun/jgkq,kgcq->gcjq/dot_general | solution.py:127
  140.9 18.6 %conditional.4 = (f32[8,128,64]{1,2,0:T(8,128)S(1)}, f32[8,128,64]{1,2,0:T(8,128)S(1)}, f32[1,8,8,8,64]{2,3,4,1,0:T(8,128)}) conditional(s32[]{:T(128)} %convert_element_type.412, (f32[8,128,64]{1,2,0:T(8,128)S(1)}, f32[8,128,64]{1,2,0:T(8,128)S(1)}) %tuple.139, (s32[]{:T(128)}, s32[8]{0:T(128)S(1)}, s32[8,1,1]{0,2,1:T(1,128)S(1)}, ...), branch_computations={%region_3.3_spmd, %region_4.4_spmd.clone} | conditional | flops 53850800 | bytes 11276004 | solution.py:136
  142.7 3.6 %fusion.11 = (f32[8,128,64]{1,2,0:T(8,128)S(1)}, f32[8,128,64]{1,2,0:T(8,128)S(1)}, f32[8,128,64]{1,2,0:T(8,128)S(1)}, f32[8,128,64]{1,2,0:T(8,128)S(1)}, f32[8,...) fusion(f32[128]{0:T(128)S(1)} %get-tuple-element.437, ...), kind=kLoop, calls=%fused_computation.9 | loop fusion | flops 3473408 | bytes 2684416 | tf_op jit(solution)/shard_map/while/body/eval_jaxpr/cond/branch_1_fun/jit(_where)/select_n | solution.py:91
  146.3 6.2 %stack.51 = f32[8,8,128,64]{2,0,3,1:T(8,128)} concatenate(f32[1,8,128,64]{2,0,3,1:T(1,128)} %bitcast.229, f32[1,8,128,64]{2,0,3,1:T(1,128)} %bitcast.228, f32[1,8,128,64]{2,0,3,1:T(1,128)} %bitcast.227, f32[1,8,128,64]{2,0,3,1:T(1,128)S(1)} %bitcast.226, f32[1,8,128,64]{2,0,3,1:T(1,128)S(1)} %bitcast.225, f32[1,8,128,64]{2,0,3,1:T(1,128)S(1)} %bitcast.224, ...), dimensions={0} | concatenate | bytes 4194304 | tf_op jit(solution)/shard_map/while/body/eval_jaxpr/cond/branch_1_fun/stack | solution.py:126
  152.5 6.9 %convolution_bitcast_fusion = f32[1,8,8,8,64]{2,3,4,1,0:T(8,128)} fusion(f32[8,8,128,64]{2,0,3,1:T(8,128)} %stack.51, f32[128,8,8,64]{0,2,3,1:T(8,128)} %get-tuple-element.428), kind=kOutput, calls=%fused_computation.4 | convolution fusion | flops 50331648 | bytes 4325376 | tf_op jit(solution)/shard_map/while/body/eval_jaxpr/cond/branch_1_fun/jgkq,kgcq->gcjq/dot_general | solution.py:127
  159.5 3.1 constant_dynamic-update-slice_fusion.2
  163.7 18.6 %conditional.4 = (f32[8,128,64]{1,2,0:T(8,128)S(1)}, f32[8,128,64]{1,2,0:T(8,128)S(1)}, f32[1,8,8,8,64]{2,3,4,1,0:T(8,128)}) conditional(s32[]{:T(128)} %convert_element_type.412, (f32[8,128,64]{1,2,0:T(8,128)S(1)}, f32[8,128,64]{1,2,0:T(8,128)S(1)}) %tuple.139, (s32[]{:T(128)}, s32[8]{0:T(128)S(1)}, s32[8,1,1]{0,2,1:T(1,128)S(1)}, ...), branch_computations={%region_3.3_spmd, %region_4.4_spmd.clone} | conditional | flops 53850800 | bytes 11276004 | solution.py:136
  165.5 3.6 %fusion.11 = (f32[8,128,64]{1,2,0:T(8,128)S(1)}, f32[8,128,64]{1,2,0:T(8,128)S(1)}, f32[8,128,64]{1,2,0:T(8,128)S(1)}, f32[8,128,64]{1,2,0:T(8,128)S(1)}, f32[8,...) fusion(f32[128]{0:T(128)S(1)} %get-tuple-element.437, ...), kind=kLoop, calls=%fused_computation.9 | loop fusion | flops 3473408 | bytes 2684416 | tf_op jit(solution)/shard_map/while/body/eval_jaxpr/cond/branch_1_fun/jit(_where)/select_n | solution.py:91
  169.1 6.2 %stack.51 = f32[8,8,128,64]{2,0,3,1:T(8,128)} concatenate(f32[1,8,128,64]{2,0,3,1:T(1,128)} %bitcast.229, f32[1,8,128,64]{2,0,3,1:T(1,128)} %bitcast.228, f32[1,8,128,64]{2,0,3,1:T(1,128)} %bitcast.227, f32[1,8,128,64]{2,0,3,1:T(1,128)S(1)} %bitcast.226, f32[1,8,128,64]{2,0,3,1:T(1,128)S(1)} %bitcast.225, f32[1,8,128,64]{2,0,3,1:T(1,128)S(1)} %bitcast.224, ...), dimensions={0} | concatenate | bytes 4194304 | tf_op jit(solution)/shard_map/while/body/eval_jaxpr/cond/branch_1_fun/stack | solution.py:126
  175.3 6.9 %convolution_bitcast_fusion = f32[1,8,8,8,64]{2,3,4,1,0:T(8,128)} fusion(f32[8,8,128,64]{2,0,3,1:T(8,128)} %stack.51, f32[128,8,8,64]{0,2,3,1:T(8,128)} %get-tuple-element.428), kind=kOutput, calls=%fused_computation.4 | convolution fusion | flops 50331648 | bytes 4325376 | tf_op jit(solution)/shard_map/while/body/eval_jaxpr/cond/branch_1_fun/jgkq,kgcq->gcjq/dot_general | solution.py:127
  182.3 3.1 constant_dynamic-update-slice_fusion.2
  186.5 18.6 %conditional.4 = (f32[8,128,64]{1,2,0:T(8,128)S(1)}, f32[8,128,64]{1,2,0:T(8,128)S(1)}, f32[1,8,8,8,64]{2,3,4,1,0:T(8,128)}) conditional(s32[]{:T(128)} %convert_element_type.412, (f32[8,128,64]{1,2,0:T(8,128)S(1)}, f32[8,128,64]{1,2,0:T(8,128)S(1)}) %tuple.139, (s32[]{:T(128)}, s32[8]{0:T(128)S(1)}, s32[8,1,1]{0,2,1:T(1,128)S(1)}, ...), branch_computations={%region_3.3_spmd, %region_4.4_spmd.clone} | conditional | flops 53850800 | bytes 11276004 | solution.py:136
  188.4 3.6 %fusion.11 = (f32[8,128,64]{1,2,0:T(8,128)S(1)}, f32[8,128,64]{1,2,0:T(8,128)S(1)}, f32[8,128,64]{1,2,0:T(8,128)S(1)}, f32[8,128,64]{1,2,0:T(8,128)S(1)}, f32[8,...) fusion(f32[128]{0:T(128)S(1)} %get-tuple-element.437, ...), kind=kLoop, calls=%fused_computation.9 | loop fusion | flops 3473408 | bytes 2684416 | tf_op jit(solution)/shard_map/while/body/eval_jaxpr/cond/branch_1_fun/jit(_where)/select_n | solution.py:91
  191.9 6.2 %stack.51 = f32[8,8,128,64]{2,0,3,1:T(8,128)} concatenate(f32[1,8,128,64]{2,0,3,1:T(1,128)} %bitcast.229, f32[1,8,128,64]{2,0,3,1:T(1,128)} %bitcast.228, f32[1,8,128,64]{2,0,3,1:T(1,128)} %bitcast.227, f32[1,8,128,64]{2,0,3,1:T(1,128)S(1)} %bitcast.226, f32[1,8,128,64]{2,0,3,1:T(1,128)S(1)} %bitcast.225, f32[1,8,128,64]{2,0,3,1:T(1,128)S(1)} %bitcast.224, ...), dimensions={0} | concatenate | bytes 4194304 | tf_op jit(solution)/shard_map/while/body/eval_jaxpr/cond/branch_1_fun/stack | solution.py:126
  198.2 6.9 %convolution_bitcast_fusion = f32[1,8,8,8,64]{2,3,4,1,0:T(8,128)} fusion(f32[8,8,128,64]{2,0,3,1:T(8,128)} %stack.51, f32[128,8,8,64]{0,2,3,1:T(8,128)} %get-tuple-element.428), kind=kOutput, calls=%fused_computation.4 | convolution fusion | flops 50331648 | bytes 4325376 | tf_op jit(solution)/shard_map/while/body/eval_jaxpr/cond/branch_1_fun/jgkq,kgcq->gcjq/dot_general | solution.py:127
  205.1 3.1 constant_dynamic-update-slice_fusion.2
  209.4 18.6 %conditional.4 = (f32[8,128,64]{1,2,0:T(8,128)S(1)}, f32[8,128,64]{1,2,0:T(8,128)S(1)}, f32[1,8,8,8,64]{2,3,4,1,0:T(8,128)}) conditional(s32[]{:T(128)} %convert_element_type.412, (f32[8,128,64]{1,2,0:T(8,128)S(1)}, f32[8,128,64]{1,2,0:T(8,128)S(1)}) %tuple.139, (s32[]{:T(128)}, s32[8]{0:T(128)S(1)}, s32[8,1,1]{0,2,1:T(1,128)S(1)}, ...), branch_computations={%region_3.3_spmd, %region_4.4_spmd.clone} | conditional | flops 53850800 | bytes 11276004 | solution.py:136
  211.2 3.6 %fusion.11 = (f32[8,128,64]{1,2,0:T(8,128)S(1)}, f32[8,128,64]{1,2,0:T(8,128)S(1)}, f32[8,128,64]{1,2,0:T(8,128)S(1)}, f32[8,128,64]{1,2,0:T(8,128)S(1)}, f32[8,...) fusion(f32[128]{0:T(128)S(1)} %get-tuple-element.437, ...), kind=kLoop, calls=%fused_computation.9 | loop fusion | flops 3473408 | bytes 2684416 | tf_op jit(solution)/shard_map/while/body/eval_jaxpr/cond/branch_1_fun/jit(_where)/select_n | solution.py:91
  214.8 6.2 %stack.51 = f32[8,8,128,64]{2,0,3,1:T(8,128)} concatenate(f32[1,8,128,64]{2,0,3,1:T(1,128)} %bitcast.229, f32[1,8,128,64]{2,0,3,1:T(1,128)} %bitcast.228, f32[1,8,128,64]{2,0,3,1:T(1,128)} %bitcast.227, f32[1,8,128,64]{2,0,3,1:T(1,128)S(1)} %bitcast.226, f32[1,8,128,64]{2,0,3,1:T(1,128)S(1)} %bitcast.225, f32[1,8,128,64]{2,0,3,1:T(1,128)S(1)} %bitcast.224, ...), dimensions={0} | concatenate | bytes 4194304 | tf_op jit(solution)/shard_map/while/body/eval_jaxpr/cond/branch_1_fun/stack | solution.py:126
  221.0 6.9 %convolution_bitcast_fusion = f32[1,8,8,8,64]{2,3,4,1,0:T(8,128)} fusion(f32[8,8,128,64]{2,0,3,1:T(8,128)} %stack.51, f32[128,8,8,64]{0,2,3,1:T(8,128)} %get-tuple-element.428), kind=kOutput, calls=%fused_computation.4 | convolution fusion | flops 50331648 | bytes 4325376 | tf_op jit(solution)/shard_map/while/body/eval_jaxpr/cond/branch_1_fun/jgkq,kgcq->gcjq/dot_general | solution.py:127
  232.2 18.6 %conditional.4 = (f32[8,128,64]{1,2,0:T(8,128)S(1)}, f32[8,128,64]{1,2,0:T(8,128)S(1)}, f32[1,8,8,8,64]{2,3,4,1,0:T(8,128)}) conditional(s32[]{:T(128)} %convert_element_type.412, (f32[8,128,64]{1,2,0:T(8,128)S(1)}, f32[8,128,64]{1,2,0:T(8,128)S(1)}) %tuple.139, (s32[]{:T(128)}, s32[8]{0:T(128)S(1)}, s32[8,1,1]{0,2,1:T(1,128)S(1)}, ...), branch_computations={%region_3.3_spmd, %region_4.4_spmd.clone} | conditional | flops 53850800 | bytes 11276004 | solution.py:136
  234.0 3.6 %fusion.11 = (f32[8,128,64]{1,2,0:T(8,128)S(1)}, f32[8,128,64]{1,2,0:T(8,128)S(1)}, f32[8,128,64]{1,2,0:T(8,128)S(1)}, f32[8,128,64]{1,2,0:T(8,128)S(1)}, f32[8,...) fusion(f32[128]{0:T(128)S(1)} %get-tuple-element.437, ...), kind=kLoop, calls=%fused_computation.9 | loop fusion | flops 3473408 | bytes 2684416 | tf_op jit(solution)/shard_map/while/body/eval_jaxpr/cond/branch_1_fun/jit(_where)/select_n | solution.py:91
  237.6 6.2 %stack.51 = f32[8,8,128,64]{2,0,3,1:T(8,128)} concatenate(f32[1,8,128,64]{2,0,3,1:T(1,128)} %bitcast.229, f32[1,8,128,64]{2,0,3,1:T(1,128)} %bitcast.228, f32[1,8,128,64]{2,0,3,1:T(1,128)} %bitcast.227, f32[1,8,128,64]{2,0,3,1:T(1,128)S(1)} %bitcast.226, f32[1,8,128,64]{2,0,3,1:T(1,128)S(1)} %bitcast.225, f32[1,8,128,64]{2,0,3,1:T(1,128)S(1)} %bitcast.224, ...), dimensions={0} | concatenate | bytes 4194304 | tf_op jit(solution)/shard_map/while/body/eval_jaxpr/cond/branch_1_fun/stack | solution.py:126
  243.8 6.9 %convolution_bitcast_fusion = f32[1,8,8,8,64]{2,3,4,1,0:T(8,128)} fusion(f32[8,8,128,64]{2,0,3,1:T(8,128)} %stack.51, f32[128,8,8,64]{0,2,3,1:T(8,128)} %get-tuple-element.428), kind=kOutput, calls=%fused_computation.4 | convolution fusion | flops 50331648 | bytes 4325376 | tf_op jit(solution)/shard_map/while/body/eval_jaxpr/cond/branch_1_fun/jgkq,kgcq->gcjq/dot_general | solution.py:127
  250.8 3.1 constant_dynamic-update-slice_fusion.2
  255.0 18.6 %conditional.4 = (f32[8,128,64]{1,2,0:T(8,128)S(1)}, f32[8,128,64]{1,2,0:T(8,128)S(1)}, f32[1,8,8,8,64]{2,3,4,1,0:T(8,128)}) conditional(s32[]{:T(128)} %convert_element_type.412, (f32[8,128,64]{1,2,0:T(8,128)S(1)}, f32[8,128,64]{1,2,0:T(8,128)S(1)}) %tuple.139, (s32[]{:T(128)}, s32[8]{0:T(128)S(1)}, s32[8,1,1]{0,2,1:T(1,128)S(1)}, ...), branch_computations={%region_3.3_spmd, %region_4.4_spmd.clone} | conditional | flops 53850800 | bytes 11276004 | solution.py:136
  256.8 3.6 %fusion.11 = (f32[8,128,64]{1,2,0:T(8,128)S(1)}, f32[8,128,64]{1,2,0:T(8,128)S(1)}, f32[8,128,64]{1,2,0:T(8,128)S(1)}, f32[8,128,64]{1,2,0:T(8,128)S(1)}, f32[8,...) fusion(f32[128]{0:T(128)S(1)} %get-tuple-element.437, ...), kind=kLoop, calls=%fused_computation.9 | loop fusion | flops 3473408 | bytes 2684416 | tf_op jit(solution)/shard_map/while/body/eval_jaxpr/cond/branch_1_fun/jit(_where)/select_n | solution.py:91
  260.4 6.2 %stack.51 = f32[8,8,128,64]{2,0,3,1:T(8,128)} concatenate(f32[1,8,128,64]{2,0,3,1:T(1,128)} %bitcast.229, f32[1,8,128,64]{2,0,3,1:T(1,128)} %bitcast.228, f32[1,8,128,64]{2,0,3,1:T(1,128)} %bitcast.227, f32[1,8,128,64]{2,0,3,1:T(1,128)S(1)} %bitcast.226, f32[1,8,128,64]{2,0,3,1:T(1,128)S(1)} %bitcast.225, f32[1,8,128,64]{2,0,3,1:T(1,128)S(1)} %bitcast.224, ...), dimensions={0} | concatenate | bytes 4194304 | tf_op jit(solution)/shard_map/while/body/eval_jaxpr/cond/branch_1_fun/stack | solution.py:126
  266.7 6.9 %convolution_bitcast_fusion = f32[1,8,8,8,64]{2,3,4,1,0:T(8,128)} fusion(f32[8,8,128,64]{2,0,3,1:T(8,128)} %stack.51, f32[128,8,8,64]{0,2,3,1:T(8,128)} %get-tuple-element.428), kind=kOutput, calls=%fused_computation.4 | convolution fusion | flops 50331648 | bytes 4325376 | tf_op jit(solution)/shard_map/while/body/eval_jaxpr/cond/branch_1_fun/jgkq,kgcq->gcjq/dot_general | solution.py:127
  276.7 11.1 %copy.62 = f32[8,8,8,8,64]{4,3,2,1,0:T(8,128)} copy(f32[8,8,8,8,64]{1,3,4,0,2:T(8,128)} %bitcast.221) | data formatting | bytes 2097152 | tf_op jit(solution)/shard_map/transpose | solution.py:144
  287.8 8.5 %multiply_reduce_fusion = f32[8,8,8]{0,2,1:T(8,128)S(1)} fusion(f32[64]{0:T(128)S(1)} %compare_select_fusion.9, f32[8,8]{1,0:T(8,128)S(1)} %sqrt_multiply_fusion, f32[8,8,8,8,64]{2,3,4,1,0:T(8,128)} %get-tuple-element.216), kind=kLoop, calls=%fused_computation.97 | loop fusion | flops 1048064 | bytes 1051136 | tf_op jit(solution)/shard_map/reduce_sum | solution.py:152
  296.5 45.8 %psum.7 = f32[4,64]{1,0:T(4,128)} all-reduce(f32[4,64]{1,0:T(4,128)S(1)} %broadcast_divide_fusion), channel_id=1, replica_groups=mesh['beta'=16,'grp'=2] {'beta'}, use_global_device_ids=true, to_apply=%region_8.9 | all-reduce | flops 256 | bytes 2048 | tf_op jit(solution)/shard_map/psum | solution.py:179
  342.3 3.3 broadcast_multiply_fusion
  (280 shorter events, 39.6 us)
Async XLA Ops:
  0.6 1.6 copy-start
  18.8 51.5 %all-to-all-start = ((f32[16,1,32768]{2,1,0:T(1,128)}), f32[16,1,32768]{2,1,0:T(1,128)}, u32[]{:S(2)}, u32[]{:S(2)}) async-start(f32[16,1,32768]{2,1,0:T(1,128)} %reshape.2457), calls=%async_computation | async-start | bytes 4194304 | tf_op jit(solution)/shard_map/all_to_all | solution.py:173
  94.1 1.1 copy-start.2
  113.8 3.1 copy-start.3
  116.9 1.1 copy-start.2
  136.7 3.1 copy-start.3
  139.7 1.1 copy-start.2
  159.5 3.1 copy-start.3
  162.6 1.1 copy-start.2
  182.3 3.1 copy-start.3
  185.4 1.1 copy-start.2
  205.1 3.1 copy-start.3
  208.3 1.1 copy-start.2
  228.0 3.1 copy-start.3
  231.1 1.1 copy-start.2
  250.8 3.1 copy-start.3
  253.9 1.1 copy-start.2
  273.6 3.0 copy-start.3
  287.8 8.7 %copy-start.1 = (f32[64]{0:T(128)S(1)}, f32[64]{0:T(128)}, u32[]{:S(2)}) copy-start(f32[64]{0:T(128)} %fusion.87) | copy-start | bytes 772
where the time goes:
time: 351 us; the launch traced here: 346 us
  local copies, waits for them, and re-layouts  117 us (33%)
  other arithmetic  62.1 us (18%)
  matrix products  59.5 us (17%)
  blocking collectives  45.8 us (13%)
  waiting for transfers between devices  38.1 us (11%)
  loops' own time  11.6 us (3%)
  starting transfers between devices  8.4 us (2%)
  between operations  3.57 us (1%)
    dot_general x8, matrix products, compute_block(): jnp.einsum('jgkq,kgcq->gcjq', stacked, weighted, precision=HIGHEST)  55.6 us
    another operation x8, local copies, waits for them, and re-layouts, compute_block(): stacked = jnp.stack(levels, axis=0)  49.9 us
    psum x1, blocking collectives, local(): power = lax.psum(power_part, 'beta')  45.8 us
    all_to_all x1, waiting for transfers between devices, local(): lax.all_to_all(spectrum, 'beta', split_axis=1, concat_axis=0, tiled=True)  38.1 us
    select_n x8, other arithmetic, advance(): renewed = jnp.where(degree == lowest, start_value, recurred)  28.7 us
    dynamic_update_slice x8, local copies, waits for them, and re-layouts, degree_rows(): lax.scan(block_step, (empty_state, empty_state), jnp.arange(block_count,...  24.7 us
    unnamed x7, local copies, waits for them, and re-layouts  15.6 us
    transpose x1, local copies, waits for them, and re-layouts, degree_rows(): jnp.transpose(parts, (1, 2, 0, 3, 4))  11.1 us
  transfers between devices with their start and end apart: 1, of which 1 were waited for; matrix products, arithmetic and copies ran while one was open for 1% of the time, Pallas kernels for 0%

commit v1 on v0

--- a/solution.py
+++ b/solution.py
@@ -176,7 +176,9 @@
     computed = degree_rows(owned_rows, weighted, spread)
     power_part = degree_energy(computed, functions, spread)
     coeffs = computed
-    power = lax.psum(power_part, "beta")
+    power = power_part
+    for hop in (1, 2, 4, 8):
+        power = power + lax.ppermute(power, "beta", [(dev, dev ^ hop) for dev in range(16)])
     coeffs = coeffs.reshape(row_count, 2, functions, spread, spread)
     return (coeffs, power)
 

time: 351 us -> 321 us (0.915)
  blocking collectives: 45.8 us -> 0 us
  waiting for transfers between devices: 38.1 us -> 46.2 us
  starting transfers between devices: 8.4 us -> 14.8 us
    psum x1 -> x0, blocking collectives: 45.8 us -> none  [local(): power = lax.psum(power_part, 'beta')]
    ppermute x0 -> x4, waiting for transfers between devices: none -> 7.16 us  [local(): lax.ppermute(power, 'beta', [(dev, dev ^ hop) for dev in range(16)])]
    ppermute x0 -> x4, starting transfers between devices: none -> 6.41 us  [local(): lax.ppermute(power, 'beta', [(dev, dev ^ hop) for dev in range(16)])]
    unnamed x7 -> x5, local copies, waits for them, and re-layouts: 15.6 us -> 15.6 us
  transfers between devices with their start and end apart: 1 -> 5, of which waited for: 1 -> 3; matrix products, arithmetic and copies ran while one was open for 1% -> 5% of each run, Pallas kernels for 0% -> 0%
where the time goes in v1:
time: 321 us; the launch traced here: 315 us
  local copies, waits for them, and re-layouts  117 us (36%)
  other arithmetic  61.8 us (19%)
  matrix products  59.4 us (19%)
  waiting for transfers between devices  46.2 us (14%)
  starting transfers between devices  14.8 us (5%)
  loops' own time  12.9 us (4%)
  between operations  3.31 us (1%)
    dot_general x8, matrix products, compute_block(): jnp.einsum('jgkq,kgcq->gcjq', stacked, weighted, precision=HIGHEST)  55.5 us
    another operation x8, local copies, waits for them, and re-layouts, compute_block(): stacked = jnp.stack(levels, axis=0)  50 us
    all_to_all x1, waiting for transfers between devices, local(): lax.all_to_all(spectrum, 'beta', split_axis=1, concat_axis=0, tiled=True)  39 us
    select_n x8, other arithmetic, advance(): renewed = jnp.where(degree == lowest, start_value, recurred)  28.4 us
    dynamic_update_slice x8, local copies, waits for them, and re-layouts, degree_rows(): lax.scan(block_step, (empty_state, empty_state), jnp.arange(block_count,...  24.7 us
    unnamed x5, local copies, waits for them, and re-layouts  15.6 us
    transpose x1, local copies, waits for them, and re-layouts, degree_rows(): jnp.transpose(parts, (1, 2, 0, 3, 4))  11.1 us
    all_to_all x1, other arithmetic, local(): lax.all_to_all(spectrum, 'beta', split_axis=1, concat_axis=0, tiled=True)  8.58 us
  transfers between devices with their start and end apart: 5, of which 3 were waited for; matrix products, arithmetic and copies ran while one was open for 5% of the time, Pallas kernels for 0%

profile of v1, /device:TPU:0, one launch (start us, length us, event | category | flops | bytes accessed | tf_op | source)
XLA Modules:
  0.0 315.3 jit_solution(262321723986800368)
XLA Ops:
  7.7 5.6 %copy.58 = f32[8,128,8,64]{3,2,0,1:T(8,128)} copy(f32[8,128,8,64]{1,3,2,0:T(8,128)} %bitcast.233) | data formatting | bytes 4194304 | tf_op jit(solution)/shard_map/reshape | solution.py:172
  13.3 5.5 %reshape.2457 = f32[16,1,32768]{2,1,0:T(1,128)} reshape(f32[128,8,8,64]{3,2,1,0:T(8,128)} %bitcast.230) | data formatting | bytes 4194304
  18.8 8.4 %all-to-all-start = ((f32[16,1,32768]{2,1,0:T(1,128)}), f32[16,1,32768]{2,1,0:T(1,128)}, u32[]{:S(2)}, u32[]{:S(2)}) async-start(f32[16,1,32768]{2,1,0:T(1,128)} %reshape.2457), calls=%async_computation | async-start | bytes 4194304 | tf_op jit(solution)/shard_map/all_to_all | solution.py:173
  31.3 39.0 %all-to-all-done = f32[16,1,32768]{2,1,0:T(1,128)} async-done(((f32[16,1,32768]{2,1,0:T(1,128)}), f32[16,1,32768]{2,1,0:T(1,128)}, u32[]{:S(2)}, u32[]{:S(2)}) %all-to-all-start) | async-done | bytes 2097184 | tf_op jit(solution)/shard_map/all_to_all | solution.py:173
  70.8 8.6 %reduce.3 = f32[16,32768]{1,0:T(8,128)} reduce(f32[16,1,32768]{2,1,0:T(1,128)} %all-to-all-done, f32[]{:T(128)} %broadcast.2681), dimensions={1}, to_apply=%all_to_all.13.reduce_sub_computation | reduce | bytes 4194308 | tf_op jit(solution)/shard_map/all_to_all | solution.py:173
  79.4 4.2 %reshape.2458 = f32[128,8,8,64]{3,2,1,0:T(8,128)} reshape(f32[16,32768]{1,0:T(8,128)} %reduce.3) | data formatting | bytes 4194304
  88.7 5.0 %copy.61 = f32[128,8,8,64]{0,2,3,1:T(8,128)} copy(f32[128,8,8,64]{3,2,1,0:T(8,128)} %bitcast_multiply_fusion) | data formatting | bytes 4194304
  93.8 184.2 %while.16 = (s32[]{:T(128)}, f32[8,128,64]{1,2,0:T(8,128)S(1)}, f32[8,128,64]{1,2,0:T(8,128)S(1)}, f32[8,8,8,8,64]{2,3,4,1,0:T(8,128)}, s32[8]{0:T(128)S(1)}, /*...) while((s32[]{:T(128)}, f32[8,128,64]{1,2,0:T(8,128)S(1)}, ...), condition=%wide.region_5.6_spmd.clone.clone, body=%wide.region_2.5_spmd.clone.clone.sunk | while | flops 53850804 | bytes 15474387 | solution.py:141
  95.3 18.6 %conditional.4 = (f32[8,128,64]{1,2,0:T(8,128)S(1)}, f32[8,128,64]{1,2,0:T(8,128)S(1)}, f32[1,8,8,8,64]{2,3,4,1,0:T(8,128)}) conditional(s32[]{:T(128)} %convert_element_type.412, (f32[8,128,64]{1,2,0:T(8,128)S(1)}, f32[8,128,64]{1,2,0:T(8,128)S(1)}) %tuple.139, (s32[]{:T(128)}, s32[8]{0:T(128)S(1)}, s32[8,1,1]{0,2,1:T(1,128)S(1)}, ...), branch_computations={%region_3.3_spmd, %region_4.4_spmd.clone} | conditional | flops 53850800 | bytes 11276004 | solution.py:136
  97.2 3.6 %fusion.11 = (f32[8,128,64]{1,2,0:T(8,128)S(1)}, f32[8,128,64]{1,2,0:T(8,128)S(1)}, f32[8,128,64]{1,2,0:T(8,128)S(1)}, f32[8,128,64]{1,2,0:T(8,128)S(1)}, f32[8,...) fusion(f32[128]{0:T(128)S(1)} %get-tuple-element.437, ...), kind=kLoop, calls=%fused_computation.9 | loop fusion | flops 3473408 | bytes 2684416 | tf_op jit(solution)/shard_map/while/body/eval_jaxpr/cond/branch_1_fun/jit(_where)/select_n | solution.py:91
  100.7 6.3 %stack.51 = f32[8,8,128,64]{2,0,3,1:T(8,128)} concatenate(f32[1,8,128,64]{2,0,3,1:T(1,128)} %bitcast.229, f32[1,8,128,64]{2,0,3,1:T(1,128)} %bitcast.228, f32[1,8,128,64]{2,0,3,1:T(1,128)} %bitcast.227, f32[1,8,128,64]{2,0,3,1:T(1,128)S(1)} %bitcast.226, f32[1,8,128,64]{2,0,3,1:T(1,128)S(1)} %bitcast.225, f32[1,8,128,64]{2,0,3,1:T(1,128)S(1)} %bitcast.224, ...), dimensions={0} | concatenate | bytes 4194304 | tf_op jit(solution)/shard_map/while/body/eval_jaxpr/cond/branch_1_fun/stack | solution.py:126
  107.0 6.9 %convolution_bitcast_fusion = f32[1,8,8,8,64]{2,3,4,1,0:T(8,128)} fusion(f32[8,8,128,64]{2,0,3,1:T(8,128)} %stack.51, f32[128,8,8,64]{0,2,3,1:T(8,128)} %get-tuple-element.428), kind=kOutput, calls=%fused_computation.4 | convolution fusion | flops 50331648 | bytes 4325376 | tf_op jit(solution)/shard_map/while/body/eval_jaxpr/cond/branch_1_fun/jgkq,kgcq->gcjq/dot_general | solution.py:127
  118.3 18.6 %conditional.4 = (f32[8,128,64]{1,2,0:T(8,128)S(1)}, f32[8,128,64]{1,2,0:T(8,128)S(1)}, f32[1,8,8,8,64]{2,3,4,1,0:T(8,128)}) conditional(s32[]{:T(128)} %convert_element_type.412, (f32[8,128,64]{1,2,0:T(8,128)S(1)}, f32[8,128,64]{1,2,0:T(8,128)S(1)}) %tuple.139, (s32[]{:T(128)}, s32[8]{0:T(128)S(1)}, s32[8,1,1]{0,2,1:T(1,128)S(1)}, ...), branch_computations={%region_3.3_spmd, %region_4.4_spmd.clone} | conditional | flops 53850800 | bytes 11276004 | solution.py:136
  120.2 3.6 %fusion.11 = (f32[8,128,64]{1,2,0:T(8,128)S(1)}, f32[8,128,64]{1,2,0:T(8,128)S(1)}, f32[8,128,64]{1,2,0:T(8,128)S(1)}, f32[8,128,64]{1,2,0:T(8,128)S(1)}, f32[8,...) fusion(f32[128]{0:T(128)S(1)} %get-tuple-element.437, ...), kind=kLoop, calls=%fused_computation.9 | loop fusion | flops 3473408 | bytes 2684416 | tf_op jit(solution)/shard_map/while/body/eval_jaxpr/cond/branch_1_fun/jit(_where)/select_n | solution.py:91
  123.7 6.3 %stack.51 = f32[8,8,128,64]{2,0,3,1:T(8,128)} concatenate(f32[1,8,128,64]{2,0,3,1:T(1,128)} %bitcast.229, f32[1,8,128,64]{2,0,3,1:T(1,128)} %bitcast.228, f32[1,8,128,64]{2,0,3,1:T(1,128)} %bitcast.227, f32[1,8,128,64]{2,0,3,1:T(1,128)S(1)} %bitcast.226, f32[1,8,128,64]{2,0,3,1:T(1,128)S(1)} %bitcast.225, f32[1,8,128,64]{2,0,3,1:T(1,128)S(1)} %bitcast.224, ...), dimensions={0} | concatenate | bytes 4194304 | tf_op jit(solution)/shard_map/while/body/eval_jaxpr/cond/branch_1_fun/stack | solution.py:126
  130.0 6.9 %convolution_bitcast_fusion = f32[1,8,8,8,64]{2,3,4,1,0:T(8,128)} fusion(f32[8,8,128,64]{2,0,3,1:T(8,128)} %stack.51, f32[128,8,8,64]{0,2,3,1:T(8,128)} %get-tuple-element.428), kind=kOutput, calls=%fused_computation.4 | convolution fusion | flops 50331648 | bytes 4325376 | tf_op jit(solution)/shard_map/while/body/eval_jaxpr/cond/branch_1_fun/jgkq,kgcq->gcjq/dot_general | solution.py:127
  141.2 18.6 %conditional.4 = (f32[8,128,64]{1,2,0:T(8,128)S(1)}, f32[8,128,64]{1,2,0:T(8,128)S(1)}, f32[1,8,8,8,64]{2,3,4,1,0:T(8,128)}) conditional(s32[]{:T(128)} %convert_element_type.412, (f32[8,128,64]{1,2,0:T(8,128)S(1)}, f32[8,128,64]{1,2,0:T(8,128)S(1)}) %tuple.139, (s32[]{:T(128)}, s32[8]{0:T(128)S(1)}, s32[8,1,1]{0,2,1:T(1,128)S(1)}, ...), branch_computations={%region_3.3_spmd, %region_4.4_spmd.clone} | conditional | flops 53850800 | bytes 11276004 | solution.py:136
  143.1 3.6 %fusion.11 = (f32[8,128,64]{1,2,0:T(8,128)S(1)}, f32[8,128,64]{1,2,0:T(8,128)S(1)}, f32[8,128,64]{1,2,0:T(8,128)S(1)}, f32[8,128,64]{1,2,0:T(8,128)S(1)}, f32[8,...) fusion(f32[128]{0:T(128)S(1)} %get-tuple-element.437, ...), kind=kLoop, calls=%fused_computation.9 | loop fusion | flops 3473408 | bytes 2684416 | tf_op jit(solution)/shard_map/while/body/eval_jaxpr/cond/branch_1_fun/jit(_where)/select_n | solution.py:91
  146.7 6.3 %stack.51 = f32[8,8,128,64]{2,0,3,1:T(8,128)} concatenate(f32[1,8,128,64]{2,0,3,1:T(1,128)} %bitcast.229, f32[1,8,128,64]{2,0,3,1:T(1,128)} %bitcast.228, f32[1,8,128,64]{2,0,3,1:T(1,128)} %bitcast.227, f32[1,8,128,64]{2,0,3,1:T(1,128)S(1)} %bitcast.226, f32[1,8,128,64]{2,0,3,1:T(1,128)S(1)} %bitcast.225, f32[1,8,128,64]{2,0,3,1:T(1,128)S(1)} %bitcast.224, ...), dimensions={0} | concatenate | bytes 4194304 | tf_op jit(solution)/shard_map/while/body/eval_jaxpr/cond/branch_1_fun/stack | solution.py:126
  152.9 6.9 %convolution_bitcast_fusion = f32[1,8,8,8,64]{2,3,4,1,0:T(8,128)} fusion(f32[8,8,128,64]{2,0,3,1:T(8,128)} %stack.51, f32[128,8,8,64]{0,2,3,1:T(8,128)} %get-tuple-element.428), kind=kOutput, calls=%fused_computation.4 | convolution fusion | flops 50331648 | bytes 4325376 | tf_op jit(solution)/shard_map/while/body/eval_jaxpr/cond/branch_1_fun/jgkq,kgcq->gcjq/dot_general | solution.py:127
  164.2 18.7 %conditional.4 = (f32[8,128,64]{1,2,0:T(8,128)S(1)}, f32[8,128,64]{1,2,0:T(8,128)S(1)}, f32[1,8,8,8,64]{2,3,4,1,0:T(8,128)}) conditional(s32[]{:T(128)} %convert_element_type.412, (f32[8,128,64]{1,2,0:T(8,128)S(1)}, f32[8,128,64]{1,2,0:T(8,128)S(1)}) %tuple.139, (s32[]{:T(128)}, s32[8]{0:T(128)S(1)}, s32[8,1,1]{0,2,1:T(1,128)S(1)}, ...), branch_computations={%region_3.3_spmd, %region_4.4_spmd.clone} | conditional | flops 53850800 | bytes 11276004 | solution.py:136
  166.1 3.6 %fusion.11 = (f32[8,128,64]{1,2,0:T(8,128)S(1)}, f32[8,128,64]{1,2,0:T(8,128)S(1)}, f32[8,128,64]{1,2,0:T(8,128)S(1)}, f32[8,128,64]{1,2,0:T(8,128)S(1)}, f32[8,...) fusion(f32[128]{0:T(128)S(1)} %get-tuple-element.437, ...), kind=kLoop, calls=%fused_computation.9 | loop fusion | flops 3473408 | bytes 2684416 | tf_op jit(solution)/shard_map/while/body/eval_jaxpr/cond/branch_1_fun/jit(_where)/select_n | solution.py:91
  169.7 6.3 %stack.51 = f32[8,8,128,64]{2,0,3,1:T(8,128)} concatenate(f32[1,8,128,64]{2,0,3,1:T(1,128)} %bitcast.229, f32[1,8,128,64]{2,0,3,1:T(1,128)} %bitcast.228, f32[1,8,128,64]{2,0,3,1:T(1,128)} %bitcast.227, f32[1,8,128,64]{2,0,3,1:T(1,128)S(1)} %bitcast.226, f32[1,8,128,64]{2,0,3,1:T(1,128)S(1)} %bitcast.225, f32[1,8,128,64]{2,0,3,1:T(1,128)S(1)} %bitcast.224, ...), dimensions={0} | concatenate | bytes 4194304 | tf_op jit(solution)/shard_map/while/body/eval_jaxpr/cond/branch_1_fun/stack | solution.py:126
  175.9 6.9 %convolution_bitcast_fusion = f32[1,8,8,8,64]{2,3,4,1,0:T(8,128)} fusion(f32[8,8,128,64]{2,0,3,1:T(8,128)} %stack.51, f32[128,8,8,64]{0,2,3,1:T(8,128)} %get-tuple-element.428), kind=kOutput, calls=%fused_computation.4 | convolution fusion | flops 50331648 | bytes 4325376 | tf_op jit(solution)/shard_map/while/body/eval_jaxpr/cond/branch_1_fun/jgkq,kgcq->gcjq/dot_general | solution.py:127
  182.9 3.1 constant_dynamic-update-slice_fusion.2
  187.2 18.6 %conditional.4 = (f32[8,128,64]{1,2,0:T(8,128)S(1)}, f32[8,128,64]{1,2,0:T(8,128)S(1)}, f32[1,8,8,8,64]{2,3,4,1,0:T(8,128)}) conditional(s32[]{:T(128)} %convert_element_type.412, (f32[8,128,64]{1,2,0:T(8,128)S(1)}, f32[8,128,64]{1,2,0:T(8,128)S(1)}) %tuple.139, (s32[]{:T(128)}, s32[8]{0:T(128)S(1)}, s32[8,1,1]{0,2,1:T(1,128)S(1)}, ...), branch_computations={%region_3.3_spmd, %region_4.4_spmd.clone} | conditional | flops 53850800 | bytes 11276004 | solution.py:136
  189.2 3.6 %fusion.11 = (f32[8,128,64]{1,2,0:T(8,128)S(1)}, f32[8,128,64]{1,2,0:T(8,128)S(1)}, f32[8,128,64]{1,2,0:T(8,128)S(1)}, f32[8,128,64]{1,2,0:T(8,128)S(1)}, f32[8,...) fusion(f32[128]{0:T(128)S(1)} %get-tuple-element.437, ...), kind=kLoop, calls=%fused_computation.9 | loop fusion | flops 3473408 | bytes 2684416 | tf_op jit(solution)/shard_map/while/body/eval_jaxpr/cond/branch_1_fun/jit(_where)/select_n | solution.py:91
  192.7 6.3 %stack.51 = f32[8,8,128,64]{2,0,3,1:T(8,128)} concatenate(f32[1,8,128,64]{2,0,3,1:T(1,128)} %bitcast.229, f32[1,8,128,64]{2,0,3,1:T(1,128)} %bitcast.228, f32[1,8,128,64]{2,0,3,1:T(1,128)} %bitcast.227, f32[1,8,128,64]{2,0,3,1:T(1,128)S(1)} %bitcast.226, f32[1,8,128,64]{2,0,3,1:T(1,128)S(1)} %bitcast.225, f32[1,8,128,64]{2,0,3,1:T(1,128)S(1)} %bitcast.224, ...), dimensions={0} | concatenate | bytes 4194304 | tf_op jit(solution)/shard_map/while/body/eval_jaxpr/cond/branch_1_fun/stack | solution.py:126
  199.0 6.9 %convolution_bitcast_fusion = f32[1,8,8,8,64]{2,3,4,1,0:T(8,128)} fusion(f32[8,8,128,64]{2,0,3,1:T(8,128)} %stack.51, f32[128,8,8,64]{0,2,3,1:T(8,128)} %get-tuple-element.428), kind=kOutput, calls=%fused_computation.4 | convolution fusion | flops 50331648 | bytes 4325376 | tf_op jit(solution)/shard_map/while/body/eval_jaxpr/cond/branch_1_fun/jgkq,kgcq->gcjq/dot_general | solution.py:127
  205.9 3.1 constant_dynamic-update-slice_fusion.2
  210.3 18.7 %conditional.4 = (f32[8,128,64]{1,2,0:T(8,128)S(1)}, f32[8,128,64]{1,2,0:T(8,128)S(1)}, f32[1,8,8,8,64]{2,3,4,1,0:T(8,128)}) conditional(s32[]{:T(128)} %convert_element_type.412, (f32[8,128,64]{1,2,0:T(8,128)S(1)}, f32[8,128,64]{1,2,0:T(8,128)S(1)}) %tuple.139, (s32[]{:T(128)}, s32[8]{0:T(128)S(1)}, s32[8,1,1]{0,2,1:T(1,128)S(1)}, ...), branch_computations={%region_3.3_spmd, %region_4.4_spmd.clone} | conditional | flops 53850800 | bytes 11276004 | solution.py:136
  212.2 3.6 %fusion.11 = (f32[8,128,64]{1,2,0:T(8,128)S(1)}, f32[8,128,64]{1,2,0:T(8,128)S(1)}, f32[8,128,64]{1,2,0:T(8,128)S(1)}, f32[8,128,64]{1,2,0:T(8,128)S(1)}, f32[8,...) fusion(f32[128]{0:T(128)S(1)} %get-tuple-element.437, ...), kind=kLoop, calls=%fused_computation.9 | loop fusion | flops 3473408 | bytes 2684416 | tf_op jit(solution)/shard_map/while/body/eval_jaxpr/cond/branch_1_fun/jit(_where)/select_n | solution.py:91
  215.8 6.3 %stack.51 = f32[8,8,128,64]{2,0,3,1:T(8,128)} concatenate(f32[1,8,128,64]{2,0,3,1:T(1,128)} %bitcast.229, f32[1,8,128,64]{2,0,3,1:T(1,128)} %bitcast.228, f32[1,8,128,64]{2,0,3,1:T(1,128)} %bitcast.227, f32[1,8,128,64]{2,0,3,1:T(1,128)S(1)} %bitcast.226, f32[1,8,128,64]{2,0,3,1:T(1,128)S(1)} %bitcast.225, f32[1,8,128,64]{2,0,3,1:T(1,128)S(1)} %bitcast.224, ...), dimensions={0} | concatenate | bytes 4194304 | tf_op jit(solution)/shard_map/while/body/eval_jaxpr/cond/branch_1_fun/stack | solution.py:126
  222.0 6.9 %convolution_bitcast_fusion = f32[1,8,8,8,64]{2,3,4,1,0:T(8,128)} fusion(f32[8,8,128,64]{2,0,3,1:T(8,128)} %stack.51, f32[128,8,8,64]{0,2,3,1:T(8,128)} %get-tuple-element.428), kind=kOutput, calls=%fused_computation.4 | convolution fusion | flops 50331648 | bytes 4325376 | tf_op jit(solution)/shard_map/while/body/eval_jaxpr/cond/branch_1_fun/jgkq,kgcq->gcjq/dot_general | solution.py:127
  233.3 18.6 %conditional.4 = (f32[8,128,64]{1,2,0:T(8,128)S(1)}, f32[8,128,64]{1,2,0:T(8,128)S(1)}, f32[1,8,8,8,64]{2,3,4,1,0:T(8,128)}) conditional(s32[]{:T(128)} %convert_element_type.412, (f32[8,128,64]{1,2,0:T(8,128)S(1)}, f32[8,128,64]{1,2,0:T(8,128)S(1)}) %tuple.139, (s32[]{:T(128)}, s32[8]{0:T(128)S(1)}, s32[8,1,1]{0,2,1:T(1,128)S(1)}, ...), branch_computations={%region_3.3_spmd, %region_4.4_spmd.clone} | conditional | flops 53850800 | bytes 11276004 | solution.py:136
  235.2 3.6 %fusion.11 = (f32[8,128,64]{1,2,0:T(8,128)S(1)}, f32[8,128,64]{1,2,0:T(8,128)S(1)}, f32[8,128,64]{1,2,0:T(8,128)S(1)}, f32[8,128,64]{1,2,0:T(8,128)S(1)}, f32[8,...) fusion(f32[128]{0:T(128)S(1)} %get-tuple-element.437, ...), kind=kLoop, calls=%fused_computation.9 | loop fusion | flops 3473408 | bytes 2684416 | tf_op jit(solution)/shard_map/while/body/eval_jaxpr/cond/branch_1_fun/jit(_where)/select_n | solution.py:91
  238.8 6.3 %stack.51 = f32[8,8,128,64]{2,0,3,1:T(8,128)} concatenate(f32[1,8,128,64]{2,0,3,1:T(1,128)} %bitcast.229, f32[1,8,128,64]{2,0,3,1:T(1,128)} %bitcast.228, f32[1,8,128,64]{2,0,3,1:T(1,128)} %bitcast.227, f32[1,8,128,64]{2,0,3,1:T(1,128)S(1)} %bitcast.226, f32[1,8,128,64]{2,0,3,1:T(1,128)S(1)} %bitcast.225, f32[1,8,128,64]{2,0,3,1:T(1,128)S(1)} %bitcast.224, ...), dimensions={0} | concatenate | bytes 4194304 | tf_op jit(solution)/shard_map/while/body/eval_jaxpr/cond/branch_1_fun/stack | solution.py:126
  245.0 6.9 %convolution_bitcast_fusion = f32[1,8,8,8,64]{2,3,4,1,0:T(8,128)} fusion(f32[8,8,128,64]{2,0,3,1:T(8,128)} %stack.51, f32[128,8,8,64]{0,2,3,1:T(8,128)} %get-tuple-element.428), kind=kOutput, calls=%fused_computation.4 | convolution fusion | flops 50331648 | bytes 4325376 | tf_op jit(solution)/shard_map/while/body/eval_jaxpr/cond/branch_1_fun/jgkq,kgcq->gcjq/dot_general | solution.py:127
  256.3 18.7 %conditional.4 = (f32[8,128,64]{1,2,0:T(8,128)S(1)}, f32[8,128,64]{1,2,0:T(8,128)S(1)}, f32[1,8,8,8,64]{2,3,4,1,0:T(8,128)}) conditional(s32[]{:T(128)} %convert_element_type.412, (f32[8,128,64]{1,2,0:T(8,128)S(1)}, f32[8,128,64]{1,2,0:T(8,128)S(1)}) %tuple.139, (s32[]{:T(128)}, s32[8]{0:T(128)S(1)}, s32[8,1,1]{0,2,1:T(1,128)S(1)}, ...), branch_computations={%region_3.3_spmd, %region_4.4_spmd.clone} | conditional | flops 53850800 | bytes 11276004 | solution.py:136
  258.2 3.6 %fusion.11 = (f32[8,128,64]{1,2,0:T(8,128)S(1)}, f32[8,128,64]{1,2,0:T(8,128)S(1)}, f32[8,128,64]{1,2,0:T(8,128)S(1)}, f32[8,128,64]{1,2,0:T(8,128)S(1)}, f32[8,...) fusion(f32[128]{0:T(128)S(1)} %get-tuple-element.437, ...), kind=kLoop, calls=%fused_computation.9 | loop fusion | flops 3473408 | bytes 2684416 | tf_op jit(solution)/shard_map/while/body/eval_jaxpr/cond/branch_1_fun/jit(_where)/select_n | solution.py:91
  261.7 6.3 %stack.51 = f32[8,8,128,64]{2,0,3,1:T(8,128)} concatenate(f32[1,8,128,64]{2,0,3,1:T(1,128)} %bitcast.229, f32[1,8,128,64]{2,0,3,1:T(1,128)} %bitcast.228, f32[1,8,128,64]{2,0,3,1:T(1,128)} %bitcast.227, f32[1,8,128,64]{2,0,3,1:T(1,128)S(1)} %bitcast.226, f32[1,8,128,64]{2,0,3,1:T(1,128)S(1)} %bitcast.225, f32[1,8,128,64]{2,0,3,1:T(1,128)S(1)} %bitcast.224, ...), dimensions={0} | concatenate | bytes 4194304 | tf_op jit(solution)/shard_map/while/body/eval_jaxpr/cond/branch_1_fun/stack | solution.py:126
  268.0 6.9 %convolution_bitcast_fusion = f32[1,8,8,8,64]{2,3,4,1,0:T(8,128)} fusion(f32[8,8,128,64]{2,0,3,1:T(8,128)} %stack.51, f32[128,8,8,64]{0,2,3,1:T(8,128)} %get-tuple-element.428), kind=kOutput, calls=%fused_computation.4 | convolution fusion | flops 50331648 | bytes 4325376 | tf_op jit(solution)/shard_map/while/body/eval_jaxpr/cond/branch_1_fun/jgkq,kgcq->gcjq/dot_general | solution.py:127
  278.0 8.5 %multiply_reduce_fusion = f32[8,8,8]{0,2,1:T(8,128)S(1)} fusion(f32[64]{0:T(128)S(1)} %compare_select_fusion.9, f32[8,8]{1,0:T(8,128)S(1)} %sqrt_multiply_fusion, f32[8,8,8,8,64]{2,3,4,1,0:T(8,128)} %get-tuple-element.216), kind=kLoop, calls=%fused_computation.97 | loop fusion | flops 1048064 | bytes 1051136 | tf_op jit(solution)/shard_map/reduce_sum | solution.py:152
  286.8 3.6 %collective-permute-done = f32[4,64]{1,0:T(4,128)S(1)} collective-permute-done((f32[4,64]{1,0:T(4,128)S(1)}, f32[4,64]{1,0:T(4,128)S(1)}, u32[]{:S(2)}, u32[]{:S(2)}) %collective-permute-start) | collective-permute-done | bytes 1056 | tf_op jit(solution)/shard_map/ppermute | solution.py:181
  290.4 3.6 %collective-permute-done.1 = f32[4,64]{1,0:T(4,128)S(1)} collective-permute-done((f32[4,64]{1,0:T(4,128)S(1)}, f32[4,64]{1,0:T(4,128)S(1)}, u32[]{:S(2)}, u32[]{:S(2)}) %collective-permute-start.1) | collective-permute-done | bytes 1056 | tf_op jit(solution)/shard_map/ppermute | solution.py:181
  294.0 11.1 %copy.62 = f32[8,8,8,8,64]{4,3,2,1,0:T(8,128)} copy(f32[8,8,8,8,64]{1,3,4,0,2:T(8,128)} %bitcast.221) | data formatting | bytes 2097152 | tf_op jit(solution)/shard_map/transpose | solution.py:144
  305.1 6.3 %collective-permute-start.3 = (f32[4,64]{1,0:T(4,128)S(1)}, f32[4,64]{1,0:T(4,128)S(1)}, u32[]{:S(2)}, u32[]{:S(2)}) collective-permute-start(f32[4,64]{1,0:T(4,128)S(1)} %add.499), channel_id=1, source_target_pairs={{0,16},{2,18},{4,20},{6,22},{8,24},{10,26},{12,28},{14,30},{16,0},... | collective-permute-start | bytes 3080 | tf_op jit(solution)/shard_map/ppermute | solution.py:181
  311.4 3.3 %broadcast_multiply_fusion = f32[8,2,4,64,64]{4,3,2,1,0:T(8,128)} fusion(f32[8,2,4,64,64]{4,3,2,1,0:T(8,128)} %bitcast.232, f32[64]{0:T(128)S(1)} %sqrt_multiply_fusion.1), kind=kLoop, calls=%fused_computation.100 | loop fusion | flops 262144 | bytes 2097408 | tf_op jit(solution)/shard_map/mul | solution.py:146
  (289 shorter events, 46.3 us)
Async XLA Ops:
  0.6 1.6 copy-start
  18.8 51.5 %all-to-all-start = ((f32[16,1,32768]{2,1,0:T(1,128)}), f32[16,1,32768]{2,1,0:T(1,128)}, u32[]{:S(2)}, u32[]{:S(2)}) async-start(f32[16,1,32768]{2,1,0:T(1,128)} %reshape.2457), calls=%async_computation | async-start | bytes 4194304 | tf_op jit(solution)/shard_map/all_to_all | solution.py:173
  94.0 1.3 copy-start.1
  113.9 3.1 copy-start.2
  117.0 1.2 copy-start.1
  136.9 3.1 copy-start.2
  140.0 1.2 copy-start.1
  159.9 3.1 copy-start.2
  163.0 1.2 copy-start.1
  182.9 3.1 copy-start.2
  186.0 1.2 copy-start.1
  205.9 3.1 copy-start.2
  209.0 1.2 copy-start.1
  228.9 3.1 copy-start.2
  232.0 1.2 copy-start.1
  251.9 3.1 copy-start.2
  255.0 1.2 copy-start.1
  274.9 3.1 copy-start.2
  286.7 3.7 %collective-permute-start = (f32[4,64]{1,0:T(4,128)S(1)}, f32[4,64]{1,0:T(4,128)S(1)}, u32[]{:S(2)}, u32[]{:S(2)}) collective-permute-start(f32[4,64]{1,0:T(4,128)S(1)} %broadcast_divide_fusion), channel_id=1, source_target_pairs={{0,2},{2,0},{4,6},{6,4},{8,10},{10,8},{12,14},{14,12},{16,18},{18,... | collective-permute-start | bytes 3080 | tf_op jit(solution)/shard_map/ppermute | solution.py:181
  290.4 3.6 %collective-permute-start.1 = (f32[4,64]{1,0:T(4,128)S(1)}, f32[4,64]{1,0:T(4,128)S(1)}, u32[]{:S(2)}, u32[]{:S(2)}) collective-permute-start(f32[4,64]{1,0:T(4,128)S(1)} %fusion.102), channel_id=1, source_target_pairs={{0,4},{2,6},{4,0},{6,2},{8,12},{10,14},{12,8},{14,10},{16,20},{18,... | collective-permute-start | bytes 3080 | tf_op jit(solution)/shard_map/ppermute | solution.py:181
  294.0 11.1 %collective-permute-start.2 = (f32[4,64]{1,0:T(4,128)S(1)}, f32[4,64]{1,0:T(4,128)S(1)}, u32[]{:S(2)}, u32[]{:S(2)}) collective-permute-start(f32[4,64]{1,0:T(4,128)S(1)} %add.498), channel_id=1, source_target_pairs={{0,8},{2,10},{4,12},{6,14},{8,0},{10,2},{12,4},{14,6},{16,24},{18,... | collective-permute-start | bytes 3080 | tf_op jit(solution)/shard_map/ppermute | solution.py:181
  305.1 9.6 %collective-permute-start.3 = (f32[4,64]{1,0:T(4,128)S(1)}, f32[4,64]{1,0:T(4,128)S(1)}, u32[]{:S(2)}, u32[]{:S(2)}) collective-permute-start(f32[4,64]{1,0:T(4,128)S(1)} %add.499), channel_id=1, source_target_pairs={{0,16},{2,18},{4,20},{6,22},{8,24},{10,26},{12,28},{14,30},{16,0},... | collective-permute-start | bytes 3080 | tf_op jit(solution)/shard_map/ppermute | solution.py:181
